TPU v7x, 32 devices: a whole 2x2x4 slice. The times are simulated.
32 devices in a mesh: gx: 8 (over y, x, core), gy: 4 (over z).
Axes of the slice: x: 2, y: 2, z: 4, core: 2. Of those that a mesh axis runs over, the one named last changes fastest.
Arguments:
- field: float32 [65536, 512], P(('gx', 'gy')), may hold values from -6 to 6
Outputs:
- spectrum: float32 [65536, 512], P('gx', 'gy')
All inputs are finite; a program needn't handle non-finite values.
Results may differ from a plain program's by a relative error of at most 0.00007.
Values sent between devices are 32-bit elements; how exact they have to be, the bound alone decides.
A program may use at most 64 MiB of HBM per device.

v0:
```python
import math
import jax
import jax.numpy as jnp
from jax import lax
from jax.sharding import PartitionSpec as P

P_SIZE = 256
Q = 256
highest = lax.Precision.HIGHEST


def mat_dot(left, right):
    return jnp.dot(left, right, precision=highest, preferred_element_type=jnp.float32)


def finish(spec_real, spec_imag, frequency):
    length = P_SIZE * Q
    phases = math.pi / (2.0 * length) * frequency.astype(jnp.float32)
    factor = math.sqrt(2.0 / length)
    return factor * (
        jnp.cos(phases)[:, :, None] * spec_real + jnp.sin(phases)[:, :, None] * spec_imag
    )


def body(field):
    groups = lax.axis_size("gx")
    position = lax.axis_index("gx")
    length = P_SIZE * Q
    joined = lax.all_to_all(field, "gy", split_axis=1, concat_axis=0, tiled=True)
    row_count = joined.shape[0]
    col_width = joined.shape[1]
    half_rows = P_SIZE // (2 * groups)
    local_q = Q // groups
    local_p = P_SIZE // groups
    paired = joined.reshape(row_count // 2, 2, col_width)
    even_rows = paired[:, 0].reshape(half_rows, Q, col_width)
    odd_rows = jnp.flip(paired[:, 1].reshape(half_rows, Q, col_width), axis=1)
    low_half, high_half = (
        lax.all_to_all(even_rows, "gx", split_axis=1, concat_axis=0, tiled=True),
        lax.all_to_all(odd_rows, "gx", split_axis=1, concat_axis=0, tiled=True),
    )
    freq_first = jnp.arange(P_SIZE, dtype=jnp.int32)
    place_low = jnp.arange(P_SIZE // 2, dtype=jnp.int32)
    place_high = P_SIZE - 1 - place_low
    two_pi = 2.0 * math.pi
    low_phase = (
        two_pi / P_SIZE * (freq_first[:, None] * place_low[None, :] % P_SIZE).astype(jnp.float32)
    )
    high_phase = (
        two_pi / P_SIZE * (freq_first[:, None] * place_high[None, :] % P_SIZE).astype(jnp.float32)
    )
    flat_low = low_half.reshape(P_SIZE // 2, local_q * col_width)
    flat_high = high_half.reshape(P_SIZE // 2, local_q * col_width)
    cos_part = (
        mat_dot(jnp.cos(low_phase), flat_low) + mat_dot(jnp.cos(high_phase), flat_high)
    ).reshape(P_SIZE, local_q, col_width)
    sin_part = (
        mat_dot(jnp.sin(low_phase), flat_low) + mat_dot(jnp.sin(high_phase), flat_high)
    ).reshape(P_SIZE, local_q, col_width)
    part_imag = -sin_part
    second_place = position * local_q + jnp.arange(local_q, dtype=jnp.int32)
    turn_phase = (
        two_pi / length * (freq_first[:, None] * second_place[None, :] % length).astype(jnp.float32)
    )
    turn_cos = jnp.cos(turn_phase)[:, :, None]
    turn_sin = jnp.sin(turn_phase)[:, :, None]
    turned_real = cos_part * turn_cos + part_imag * turn_sin
    turned_imag = part_imag * turn_cos - cos_part * turn_sin
    moved_real, moved_imag = (
        lax.all_to_all(turned_real, "gx", split_axis=0, concat_axis=1, tiled=True),
        lax.all_to_all(turned_imag, "gx", split_axis=0, concat_axis=1, tiled=True),
    )
    second_index = jnp.arange(Q, dtype=jnp.int32)
    row_phase = two_pi / Q * (second_index[:, None] * second_index[None, :] % Q).astype(jnp.float32)
    row_cos = jnp.cos(row_phase)
    row_sin = jnp.sin(row_phase)
    spec_real = jnp.einsum("jb,kbc->jkc", row_cos, moved_real, precision=highest) + jnp.einsum(
        "jb,kbc->jkc", row_sin, moved_imag, precision=highest
    )
    spec_imag = jnp.einsum("jb,kbc->jkc", row_cos, moved_imag, precision=highest) - jnp.einsum(
        "jb,kbc->jkc", row_sin, moved_real, precision=highest
    )
    block_rows = lax.dynamic_slice_in_dim(freq_first, position * local_p, local_p, 0)
    frequency = block_rows[None, :] + P_SIZE * second_index[:, None]
    result = finish(spec_real, spec_imag, frequency)
    arrived = lax.all_to_all(result, "gx", split_axis=0, concat_axis=1, tiled=True)
    return arrived.reshape(local_q * P_SIZE, col_width)


def solution(mesh):
    in_specs = (P(("gx", "gy"), None),)
    out_specs = P("gx", "gy")
    return jax.shard_map(body, mesh=mesh, in_specs=in_specs, out_specs=out_specs, check_vma=False)
```

profile of v0, /device:TPU:0, one launch (start us, length us, event | category | flops | bytes accessed | tf_op | source)
XLA Modules:
  0.0 380.9 jit_solution(13258083812697321297)
XLA Ops:
  0.0 5.3 %copy.15 = f32[2048,512]{0,1:T(8,128)} copy(f32[2048,512]{1,0:T(8,128)} %param.1) | data formatting | bytes 8388608 | tf_op args[0]
  5.3 100.6 %all_to_all.97 = f32[2048,4,128]{0,2,1:T(8,128)} all-to-all(f32[2048,4,128]{0,2,1:T(8,128)} %bitcast.81), channel_id=1, replica_groups=mesh['gx'=8,'gy'=4] {'gy'}, dimensions={1} | all-to-all | bytes 8388608 | tf_op jit(solution)/shard_map/all_to_all | solution.py:29
  105.9 5.3 %copy.16 = f32[4,2048,128]{2,1,0:T(8,128)} copy(f32[4,2048,128]{1,2,0:T(8,128)} %bitcast.79) | data formatting | bytes 8388608 | tf_op jit(solution)/shard_map/all_to_all | solution.py:29
  111.2 7.7 %fusion.96 = (f32[4096,1,128]{2,1,0:T(1,128)}, f32[4096,1,128]{2,1,0:T(1,128)S(1)}) fusion(f32[4096,2,128]{2,1,0:T(2,128)} %bitcast.78), kind=kLoop, calls=%fused_computation.111 | loop fusion | bytes 8388608 | tf_op jit(solution)/shard_map/slice | solution.py:37
  118.9 2.5 copy.17
  121.4 3.8 all-to-all-start.1
  125.2 4.1 %copy.20 = f32[16,256,128]{2,0,1:T(8,128)} copy(f32[16,256,128]{2,1,0:T(8,128)} %bitcast.83) | data formatting | bytes 4194304 | tf_op jit(solution)/shard_map/reshape;squeeze | solution.py:37
  129.3 3.1 rev.4
  132.4 19.4 %all-to-all-done.1 = f32[16,256,128]{2,0,1:T(8,128)S(1)} async-done(((f32[16,256,128]{2,0,1:T(8,128)}), f32[16,256,128]{2,0,1:T(8,128)S(1)}, u32[]{:S(2)}, u32[]{:S(2)}) %all-to-all-start.1) | async-done | bytes 2097184 | tf_op jit(solution)/shard_map/all_to_all | solution.py:39
  151.8 4.9 %all-to-all-start.2 = ((f32[16,256,128]{2,0,1:T(8,128)}), f32[16,256,128]{2,0,1:T(8,128)}, u32[]{:S(2)}, u32[]{:S(2)}) async-start(f32[16,256,128]{2,0,1:T(8,128)} %rev.4), calls=%async_computation.2 | async-start | bytes 4194304 | tf_op jit(solution)/shard_map/all_to_all | solution.py:40
  156.7 0.5 fusion.57
  157.3 0.6 copy.19
  157.9 7.3 %fusion.9 = f32[256,4096]{1,0:T(8,128)} fusion(f32[16,8,32,128]{3,2,1,0:T(8,128)S(1)} %bitcast.73), kind=kOutput, calls=%fused_computation.16 | convolution fusion | flops 1611071488 | bytes 6291456 | tf_op jit(solution)/shard_map/dot_general | solution.py:13
  165.2 7.5 %fusion.7 = f32[256,4096]{1,0:T(8,128)} fusion(f32[16,8,32,128]{3,2,1,0:T(8,128)S(1)} %bitcast.74), kind=kOutput, calls=%fused_computation.14 | convolution fusion | flops 1611071488 | bytes 6291456 | tf_op jit(solution)/shard_map/dot_general | solution.py:13
  172.7 10.6 %all-to-all-done.2 = f32[16,256,128]{2,0,1:T(8,128)} async-done(((f32[16,256,128]{2,0,1:T(8,128)}), f32[16,256,128]{2,0,1:T(8,128)}, u32[]{:S(2)}, u32[]{:S(2)}) %all-to-all-start.2) | async-done | bytes 2097184 | tf_op jit(solution)/shard_map/all_to_all | solution.py:40
  183.3 0.0 copy-start.3
  183.3 2.4 copy.22
  185.7 0.4 copy-done.3
  186.1 4.9 %fusion.3 = f32[32,8,32,128]{3,1,2,0:T(8,128)S(1)} fusion(f32[256,4096]{1,0:T(8,128)S(1)} %copy-done.3, f32[16,8,32,128]{3,2,1,0:T(8,128)S(1)} %bitcast.75, s32[128]{0:T(128)S(1)} %iota_subtract_fusion), kind=kOutput, calls=%fused_computation.10 | convolution fusion | flops 1612120064 | bytes 10486272 | tf_op jit(solution)/shard_map/dot_general | solution.py:13
  191.1 0.0 copy-start.2
  191.1 0.8 copy.31
  191.9 1.4 copy-done.2
  193.3 5.0 %fusion.4 = f32[32,8,32,128]{3,1,2,0:T(8,128)S(1)} fusion(f32[256,4096]{1,0:T(8,128)S(1)} %copy-done.2, f32[16,8,32,128]{3,2,1,0:T(8,128)S(1)} %bitcast.76, s32[128]{0:T(128)S(1)} %iota_subtract_fusion), kind=kOutput, calls=%fused_computation.11 | convolution fusion | flops 1613168640 | bytes 10486272 | tf_op jit(solution)/shard_map/dot_general | solution.py:13
  198.2 1.0 copy.32
  199.2 4.6 %fusion.1 = (f32[256,32,128]{2,1,0:T(8,128)}, f32[256,32,128]{2,1,0:T(8,128)S(1)}) fusion(f32[32,8,32,128]{3,2,1,0:T(8,128)S(1)} %copy.32, f32[32,8,32,128]{3,2,1,0:T(8,128)S(1)} %copy.31, f32[256,32]{1,0:T(8,128)S(1)} %get-tuple-element.12, f32[256,32]{1,0:T(8,128)S(1)} %get-tuple-element.11), kind=kLoop, calls=%fused_computation.5 | loop fusion | flops 6291456 | bytes 16842752 | tf_op jit(solution)/shard_map/add | solution.py:67
  203.8 52.3 %all_to_all.98 = f32[256,32,128]{2,1,0:T(8,128)} all-to-all(f32[256,32,128]{2,1,0:T(8,128)S(1)} %get-tuple-element.6), channel_id=1, replica_groups=mesh['gx'=8,'gy'=4] {'gx'}, dimensions={0} | all-to-all | bytes 8388608 | tf_op jit(solution)/shard_map/all_to_all | solution.py:71
  256.1 4.6 %all-to-all-start.3 = ((f32[256,32,128]{2,1,0:T(8,128)}), f32[256,32,128]{2,1,0:T(8,128)}, u32[]{:S(2)}, u32[]{:S(2)}) async-start(f32[256,32,128]{2,1,0:T(8,128)} %get-tuple-element.5), calls=%async_computation.3 | async-start | bytes 8388608 | tf_op jit(solution)/shard_map/all_to_all | solution.py:70
  260.7 0.1 dynamic_slice.3
  260.8 0.2 fusion.63
  261.0 2.8 copy.24
  263.8 7.1 %fusion.19 = f32[256,32,128]{2,0,1:T(8,128)} fusion(f32[32,256,128]{2,1,0:T(8,128)S(1)} %bitcast.71), kind=kOutput, calls=%fused_computation.29 | convolution fusion | flops 3222142976 | bytes 8388608 | tf_op jit(solution)/shard_map/jb,kbc->jkc/dot_general | solution.py:77
  270.9 7.3 %fusion.21 = f32[256,32,128]{2,0,1:T(8,128)} fusion(f32[32,256,128]{2,1,0:T(8,128)S(1)} %bitcast.72), kind=kOutput, calls=%fused_computation.31 | convolution fusion | flops 3222142976 | bytes 8388608 | tf_op jit(solution)/shard_map/jb,kbc->jkc/dot_general | solution.py:80
  278.2 31.5 %all-to-all-done.3 = f32[256,32,128]{2,1,0:T(8,128)} async-done(((f32[256,32,128]{2,1,0:T(8,128)}), f32[256,32,128]{2,1,0:T(8,128)}, u32[]{:S(2)}, u32[]{:S(2)}) %all-to-all-start.3) | async-done | bytes 4194336 | tf_op jit(solution)/shard_map/all_to_all | solution.py:70
  309.8 2.8 copy.23
  312.6 0.0 copy-start
  312.6 0.0 copy-start.1
  312.6 4.8 %fusion.23 = f32[256,32,128]{2,0,1:T(8,128)S(1)} fusion(f32[32,256,128]{2,1,0:T(8,128)S(1)} %bitcast.69), kind=kOutput, calls=%fused_computation.33 | convolution fusion | flops 3222142976 | bytes 8388608 | tf_op jit(solution)/shard_map/jb,kbc->jkc/dot_general | solution.py:77
  317.4 0.0 copy-done
  317.4 0.0 copy-done.1
  317.4 6.1 %add_multiply_fusion = f32[256,32,128]{2,0,1:T(8,128)S(1)} fusion(f32[256,32,128]{2,0,1:T(8,128)S(1)} %copy-done.1, f32[256,32,128]{2,0,1:T(8,128)S(1)} %fusion.23, f32[256,32,128]{2,0,1:T(8,128)S(1)} %copy-done, f32[32,256,128]{2,1,0:T(8,128)S(1)} %bitcast.70, f32[256,32]{0,1:T(8,128)S(1)} %get-tuple-element.10, f32[256,32]{0,1:T(8,128)S(1)} %get-tuple-element.9), kind=kOutput, calls=%fused_computation.9 | convolution fusion | flops 3228434432 | bytes 21037056 | tf_op jit(solution)/shard_map/jb,kbc->jkc/dot_general | solution.py:80
  323.5 2.7 copy.25
  326.3 51.5 %all_to_all.99 = f32[256,32,128]{2,1,0:T(8,128)S(1)} all-to-all(f32[256,32,128]{2,1,0:T(8,128)S(1)} %copy.25), channel_id=1, replica_groups=mesh['gx'=8,'gy'=4] {'gx'}, dimensions={0} | all-to-all | bytes 8388608 | tf_op jit(solution)/shard_map/all_to_all | solution.py:86
  377.8 2.7 copy.26
  (4 shorter events, 0.0 us)
Async XLA Ops:
  121.4 30.4 %all-to-all-start.1 = ((f32[16,256,128]{2,0,1:T(8,128)}), f32[16,256,128]{2,0,1:T(8,128)S(1)}, u32[]{:S(2)}, u32[]{:S(2)}) async-start(f32[16,256,128]{2,0,1:T(8,128)} %copy.17), calls=%async_computation.1 | async-start | bytes 4194304 | tf_op jit(solution)/shard_map/all_to_all | solution.py:39
  151.8 31.5 %all-to-all-start.2 = ((f32[16,256,128]{2,0,1:T(8,128)}), f32[16,256,128]{2,0,1:T(8,128)}, u32[]{:S(2)}, u32[]{:S(2)}) async-start(f32[16,256,128]{2,0,1:T(8,128)} %rev.4), calls=%async_computation.2 | async-start | bytes 4194304 | tf_op jit(solution)/shard_map/all_to_all | solution.py:40
  183.3 2.8 copy-start.3
  191.1 2.2 copy-start.2
  256.1 53.7 %all-to-all-start.3 = ((f32[256,32,128]{2,1,0:T(8,128)}), f32[256,32,128]{2,1,0:T(8,128)}, u32[]{:S(2)}, u32[]{:S(2)}) async-start(f32[256,32,128]{2,1,0:T(8,128)} %get-tuple-element.5), calls=%async_computation.3 | async-start | bytes 8388608 | tf_op jit(solution)/shard_map/all_to_all | solution.py:70
  312.6 4.8 %copy-start = (f32[256,32,128]{2,0,1:T(8,128)S(1)}, f32[256,32,128]{2,0,1:T(8,128)}, u32[]{:S(2)}) copy-start(f32[256,32,128]{2,0,1:T(8,128)} %fusion.19) | copy-start | bytes 12582916
  312.6 4.8 %copy-start.1 = (f32[256,32,128]{2,0,1:T(8,128)S(1)}, f32[256,32,128]{2,0,1:T(8,128)}, u32[]{:S(2)}) copy-start(f32[256,32,128]{2,0,1:T(8,128)} %fusion.21) | copy-start | bytes 12582916
where the time goes:
time: 386 us; the launch traced here: 381 us
  blocking collectives  204 us (53%)
  waiting for transfers between devices  61.6 us (16%)
  matrix products  50 us (13%)
  local copies, waits for them, and re-layouts  45.8 us (12%)
  starting transfers between devices  13.2 us (3%)
  other arithmetic  5.36 us (1%)
    all_to_all x1, blocking collectives, body(): lax.all_to_all(field, 'gy', split_axis=1, concat_axis=0, tiled=True)  101 us
    all_to_all x1, blocking collectives, body(): lax.all_to_all(turned_imag, 'gx', split_axis=0, concat_axis=1, tiled=True)  52.3 us
    all_to_all x1, blocking collectives, body(): lax.all_to_all(result, 'gx', split_axis=0, concat_axis=1, tiled=True)  51.5 us
    all_to_all x1, waiting for transfers between devices, body(): lax.all_to_all(turned_real, 'gx', split_axis=0, concat_axis=1, tiled=True)  31.5 us
    dot_general x4, matrix products, mat_dot(): jnp.dot(left, right, precision=highest, preferred_element_type=jnp.float32)  24.7 us
    all_to_all x1, waiting for transfers between devices, body(): lax.all_to_all(even_rows, 'gx', split_axis=1, concat_axis=0, tiled=True)  19.4 us
    all_to_all x1, waiting for transfers between devices, body(): lax.all_to_all(odd_rows, 'gx', split_axis=1, concat_axis=0, tiled=True)  10.6 us
    unnamed x11, local copies, waits for them, and re-layouts  8.93 us
  transfers between devices with their start and end apart: 3, of which 3 were waited for; matrix products, arithmetic and copies ran while one was open for 11% of the time, Pallas kernels for 0%

commit v1 on v0

--- a/solution.py
+++ b/solution.py
@@ -7,6 +7,13 @@
 P_SIZE = 256
 Q = 256
 highest = lax.Precision.HIGHEST
+
+
+def _do_squares(m, dimension_no, dim_no=1):
+    odd = jnp.split(m, lax.axis_size("gx"), axis=dimension_no)
+    r_now = jnp.stack(odd, axis=0)
+    everything = lax.all_to_all(r_now, "gx", 0, 0)
+    return jnp.concatenate(everything, axis=dim_no)
 
 
 def mat_dot(left, right):
@@ -67,7 +74,7 @@
     turned_real = cos_part * turn_cos + part_imag * turn_sin
     turned_imag = part_imag * turn_cos - cos_part * turn_sin
     moved_real, moved_imag = (
-        lax.all_to_all(turned_real, "gx", split_axis=0, concat_axis=1, tiled=True),
+        _do_squares(turned_real, 0),
         lax.all_to_all(turned_imag, "gx", split_axis=0, concat_axis=1, tiled=True),
     )
     second_index = jnp.arange(Q, dtype=jnp.int32)

time: 386 us -> 388 us (level)
  blocking collectives: 204 us -> 152 us
  waiting for transfers between devices: 61.6 us -> 99.6 us
  local copies, waits for them, and re-layouts: 45.8 us -> 56.9 us
  starting transfers between devices: 13.2 us -> 17.7 us
    all_to_all x1 -> x0, blocking collectives: 52.3 us -> none  [body(): lax.all_to_all(turned_imag, 'gx', split_axis=0, concat_axis=1, tiled=True)]
    all_to_all x1 -> x2, waiting for transfers between devices: 31.5 us -> 69.6 us  [the longest x1 38 us: body(): lax.all_to_all(turned_imag, 'gx', split_axis=0, concat_axis=1, tiled=True)]
    unnamed x11 -> x20, local copies, waits for them, and re-layouts: 8.93 us -> 19.2 us
    all_to_all x1 -> x2, starting transfers between devices: 4.55 us -> 9.11 us  [the longest x1 4.56 us: _do_squares(): everything = lax.all_to_all(r_now, 'gx', 0, 0)]
  transfers between devices with their start and end apart: 3 -> 4, of which waited for: 3 -> 4; matrix products, arithmetic and copies ran while one was open for 11% -> 14% of each run, Pallas kernels for 0% -> 0%
where the time goes in v1:
time: 388 us; the launch traced here: 383 us
  blocking collectives  152 us (39%)
  waiting for transfers between devices  99.6 us (26%)
  local copies, waits for them, and re-layouts  56.9 us (15%)
  matrix products  50 us (13%)
  starting transfers between devices  17.7 us (5%)
  other arithmetic  6.11 us (2%)
    all_to_all x1, blocking collectives, body(): lax.all_to_all(field, 'gy', split_axis=1, concat_axis=0, tiled=True)  101 us
    all_to_all x1, blocking collectives, body(): lax.all_to_all(result, 'gx', split_axis=0, concat_axis=1, tiled=True)  51.5 us
    all_to_all x1, waiting for transfers between devices, body(): lax.all_to_all(turned_imag, 'gx', split_axis=0, concat_axis=1, tiled=True)  38 us
    all_to_all x1, waiting for transfers between devices, _do_squares(): everything = lax.all_to_all(r_now, 'gx', 0, 0)  31.6 us
    dot_general x4, matrix products, mat_dot(): jnp.dot(left, right, precision=highest, preferred_element_type=jnp.float32)  24.7 us
    all_to_all x1, waiting for transfers between devices, body(): lax.all_to_all(even_rows, 'gx', split_axis=1, concat_axis=0, tiled=True)  19.4 us
    unnamed x20, local copies, waits for them, and re-layouts  19.2 us
    all_to_all x1, waiting for transfers between devices, body(): lax.all_to_all(odd_rows, 'gx', split_axis=1, concat_axis=0, tiled=True)  10.6 us
  transfers between devices with their start and end apart: 4, of which 4 were waited for; matrix products, arithmetic and copies ran while one was open for 14% of the time, Pallas kernels for 0%

profile of v1, /device:TPU:0, one launch (start us, length us, event | category | flops | bytes accessed | tf_op | source)
XLA Modules:
  0.0 383.1 jit_solution(1016363120658451150)
XLA Ops:
  0.0 5.3 %copy.15 = f32[2048,512]{0,1:T(8,128)} copy(f32[2048,512]{1,0:T(8,128)} %param.1) | data formatting | bytes 8388608 | tf_op args[0]
  5.3 100.6 %all_to_all.84 = f32[2048,4,128]{0,2,1:T(8,128)} all-to-all(f32[2048,4,128]{0,2,1:T(8,128)} %bitcast.110), channel_id=1, replica_groups=mesh['gx'=8,'gy'=4] {'gy'}, dimensions={1} | all-to-all | bytes 8388608 | tf_op jit(solution)/shard_map/all_to_all | solution.py:36
  105.9 5.3 %copy.16 = f32[4,2048,128]{2,1,0:T(8,128)} copy(f32[4,2048,128]{1,2,0:T(8,128)} %bitcast.108) | data formatting | bytes 8388608 | tf_op jit(solution)/shard_map/all_to_all | solution.py:36
  111.2 7.7 %fusion.104 = (f32[4096,1,128]{2,1,0:T(1,128)}, f32[4096,1,128]{2,1,0:T(1,128)S(1)}) fusion(f32[4096,2,128]{2,1,0:T(2,128)} %bitcast.107), kind=kLoop, calls=%fused_computation.127 | loop fusion | bytes 8388608 | tf_op jit(solution)/shard_map/slice | solution.py:44
  118.9 2.5 copy.17
  121.5 3.7 all-to-all-start.1
  125.2 4.1 %copy.20 = f32[16,256,128]{2,0,1:T(8,128)} copy(f32[16,256,128]{2,1,0:T(8,128)} %bitcast.112) | data formatting | bytes 4194304 | tf_op jit(solution)/shard_map/reshape;squeeze | solution.py:44
  129.3 3.1 rev.4
  132.4 19.4 %all-to-all-done.1 = f32[16,256,128]{2,0,1:T(8,128)S(1)} async-done(((f32[16,256,128]{2,0,1:T(8,128)}), f32[16,256,128]{2,0,1:T(8,128)S(1)}, u32[]{:S(2)}, u32[]{:S(2)}) %all-to-all-start.1) | async-done | bytes 2097184 | tf_op jit(solution)/shard_map/all_to_all | solution.py:46
  151.8 4.9 %all-to-all-start.2 = ((f32[16,256,128]{2,0,1:T(8,128)}), f32[16,256,128]{2,0,1:T(8,128)}, u32[]{:S(2)}, u32[]{:S(2)}) async-start(f32[16,256,128]{2,0,1:T(8,128)} %rev.4), calls=%async_computation.2 | async-start | bytes 4194304 | tf_op jit(solution)/shard_map/all_to_all | solution.py:47
  156.7 0.5 fusion.65
  157.3 0.6 copy.19
  157.9 7.3 %fusion.9 = f32[256,4096]{1,0:T(8,128)} fusion(f32[16,8,32,128]{3,2,1,0:T(8,128)S(1)} %bitcast.103), kind=kOutput, calls=%fused_computation.16 | convolution fusion | flops 1611071488 | bytes 6291456 | tf_op jit(solution)/shard_map/dot_general | solution.py:20
  165.2 7.5 %fusion.7 = f32[256,4096]{1,0:T(8,128)} fusion(f32[16,8,32,128]{3,2,1,0:T(8,128)S(1)} %bitcast.104), kind=kOutput, calls=%fused_computation.14 | convolution fusion | flops 1611071488 | bytes 6291456 | tf_op jit(solution)/shard_map/dot_general | solution.py:20
  172.7 10.6 %all-to-all-done.2 = f32[16,256,128]{2,0,1:T(8,128)} async-done(((f32[16,256,128]{2,0,1:T(8,128)}), f32[16,256,128]{2,0,1:T(8,128)}, u32[]{:S(2)}, u32[]{:S(2)}) %all-to-all-start.2) | async-done | bytes 2097184 | tf_op jit(solution)/shard_map/all_to_all | solution.py:47
  183.3 0.0 copy-start.4
  183.3 2.4 copy.22
  185.7 0.4 copy-done.4
  186.2 4.9 %fusion.3 = f32[32,8,32,128]{3,1,2,0:T(8,128)S(1)} fusion(f32[256,4096]{1,0:T(8,128)S(1)} %copy-done.4, f32[16,8,32,128]{3,2,1,0:T(8,128)S(1)} %bitcast.105, s32[128]{0:T(128)S(1)} %iota_subtract_fusion), kind=kOutput, calls=%fused_computation.10 | convolution fusion | flops 1612120064 | bytes 10486272 | tf_op jit(solution)/shard_map/dot_general | solution.py:20
  191.1 0.0 copy-start.3
  191.1 0.8 copy.31
  191.9 1.4 copy-done.3
  193.3 5.0 %fusion.4 = f32[32,8,32,128]{3,1,2,0:T(8,128)S(1)} fusion(f32[256,4096]{1,0:T(8,128)S(1)} %copy-done.3, f32[16,8,32,128]{3,2,1,0:T(8,128)S(1)} %bitcast.106, s32[128]{0:T(128)S(1)} %iota_subtract_fusion), kind=kOutput, calls=%fused_computation.11 | convolution fusion | flops 1613168640 | bytes 10486272 | tf_op jit(solution)/shard_map/dot_general | solution.py:20
  198.3 1.0 copy.32
  199.2 5.4 %fusion.1 = (f32[256,32,128]{2,1,0:T(8,128)}, f32[256,32,128]{2,1,0:T(8,128)}) fusion(f32[32,8,32,128]{3,2,1,0:T(8,128)S(1)} %copy.32, f32[32,8,32,128]{3,2,1,0:T(8,128)S(1)} %copy.31, f32[256,32]{1,0:T(8,128)S(1)} %get-tuple-element.12, f32[256,32]{1,0:T(8,128)S(1)} %get-tuple-element.11), kind=kLoop, calls=%fused_computation.5 | loop fusion | flops 6291456 | bytes 16842752 | tf_op jit(solution)/shard_map/add | solution.py:74
  204.6 4.5 %all-to-all-start.4 = ((f32[256,32,128]{2,1,0:T(8,128)}), f32[256,32,128]{2,1,0:T(8,128)}, u32[]{:S(2)}, u32[]{:S(2)}) async-start(f32[256,32,128]{2,1,0:T(8,128)} %get-tuple-element.6), calls=%async_computation.4 | async-start | bytes 8388608 | tf_op jit(solution)/shard_map/all_to_all | solution.py:78
  209.2 0.0 copy-start.2
  209.2 2.1 fusion.22
  211.2 1.9 fusion.21
  213.1 1.9 fusion.20
  215.0 1.9 fusion.19
  216.9 0.0 copy-done.2
  216.9 0.8 fusion.18
  217.7 0.8 fusion.17
  218.6 0.8 fusion.16
  219.4 0.8 fusion.15
  220.2 38.0 %all-to-all-done.4 = f32[256,32,128]{2,1,0:T(8,128)} async-done(((f32[256,32,128]{2,1,0:T(8,128)}), f32[256,32,128]{2,1,0:T(8,128)}, u32[]{:S(2)}, u32[]{:S(2)}) %all-to-all-start.4) | async-done | bytes 4194336 | tf_op jit(solution)/shard_map/all_to_all | solution.py:78
  258.2 4.6 %all-to-all-start.3 = ((f32[8,32,32,128]{3,2,1,0:T(8,128)}), f32[8,32,32,128]{3,2,1,0:T(8,128)}, u32[]{:S(2)}, u32[]{:S(2)}) async-start(f32[8,32,32,128]{3,2,1,0:T(8,128)} %fusion.15), calls=%async_computation.3 | async-start | bytes 8388608 | tf_op jit(solution)/shard_map/all_to_all | solution.py:15
  262.8 0.1 dynamic_slice.3
  262.9 0.2 fusion.71
  263.1 2.8 copy.24
  265.9 7.1 %fusion.27 = f32[256,32,128]{2,0,1:T(8,128)} fusion(f32[32,256,128]{2,1,0:T(8,128)S(1)} %bitcast.101), kind=kOutput, calls=%fused_computation.45 | convolution fusion | flops 3222142976 | bytes 8388608 | tf_op jit(solution)/shard_map/jb,kbc->jkc/dot_general | solution.py:84
  273.1 7.3 %fusion.29 = f32[256,32,128]{2,0,1:T(8,128)} fusion(f32[32,256,128]{2,1,0:T(8,128)S(1)} %bitcast.102), kind=kOutput, calls=%fused_computation.47 | convolution fusion | flops 3222142976 | bytes 8388608 | tf_op jit(solution)/shard_map/jb,kbc->jkc/dot_general | solution.py:87
  280.4 31.6 %all-to-all-done.3 = f32[8,32,32,128]{3,2,1,0:T(8,128)} async-done(((f32[8,32,32,128]{3,2,1,0:T(8,128)}), f32[8,32,32,128]{3,2,1,0:T(8,128)}, u32[]{:S(2)}, u32[]{:S(2)}) %all-to-all-start.3) | async-done | bytes 4194336 | tf_op jit(solution)/shard_map/all_to_all | solution.py:15
  311.9 2.8 copy.23
  314.7 0.0 copy-start
  314.8 0.0 copy-start.1
  314.8 4.8 %fusion.31 = f32[256,32,128]{2,0,1:T(8,128)S(1)} fusion(f32[32,256,128]{2,1,0:T(8,128)S(1)} %bitcast.99), kind=kOutput, calls=%fused_computation.49 | convolution fusion | flops 3222142976 | bytes 8388608 | tf_op jit(solution)/shard_map/jb,kbc->jkc/dot_general | solution.py:84
  319.5 0.0 copy-done
  319.5 0.0 copy-done.1
  319.5 6.1 %add_multiply_fusion = f32[256,32,128]{2,0,1:T(8,128)S(1)} fusion(f32[256,32,128]{2,0,1:T(8,128)S(1)} %copy-done.1, f32[256,32,128]{2,0,1:T(8,128)S(1)} %fusion.31, f32[256,32,128]{2,0,1:T(8,128)S(1)} %copy-done, f32[32,256,128]{2,1,0:T(8,128)S(1)} %bitcast.100, f32[256,32]{0,1:T(8,128)S(1)} %get-tuple-element.10, f32[256,32]{0,1:T(8,128)S(1)} %get-tuple-element.9), kind=kOutput, calls=%fused_computation.9 | convolution fusion | flops 3228434432 | bytes 21037056 | tf_op jit(solution)/shard_map/jb,kbc->jkc/dot_general | solution.py:87
  325.7 2.7 copy.25
  328.4 51.5 %all_to_all.85 = f32[256,32,128]{2,1,0:T(8,128)S(1)} all-to-all(f32[256,32,128]{2,1,0:T(8,128)S(1)} %copy.25), channel_id=1, replica_groups=mesh['gx'=8,'gy'=4] {'gx'}, dimensions={0} | all-to-all | bytes 8388608 | tf_op jit(solution)/shard_map/all_to_all | solution.py:93
  379.9 2.7 copy.26
  (4 shorter events, 0.0 us)
Async XLA Ops:
  121.5 30.4 %all-to-all-start.1 = ((f32[16,256,128]{2,0,1:T(8,128)}), f32[16,256,128]{2,0,1:T(8,128)S(1)}, u32[]{:S(2)}, u32[]{:S(2)}) async-start(f32[16,256,128]{2,0,1:T(8,128)} %copy.17), calls=%async_computation.1 | async-start | bytes 4194304 | tf_op jit(solution)/shard_map/all_to_all | solution.py:46
  151.8 31.5 %all-to-all-start.2 = ((f32[16,256,128]{2,0,1:T(8,128)}), f32[16,256,128]{2,0,1:T(8,128)}, u32[]{:S(2)}, u32[]{:S(2)}) async-start(f32[16,256,128]{2,0,1:T(8,128)} %rev.4), calls=%async_computation.2 | async-start | bytes 4194304 | tf_op jit(solution)/shard_map/all_to_all | solution.py:47
  183.3 2.8 copy-start.4
  191.1 2.2 copy-start.3
  204.6 53.7 %all-to-all-start.4 = ((f32[256,32,128]{2,1,0:T(8,128)}), f32[256,32,128]{2,1,0:T(8,128)}, u32[]{:S(2)}, u32[]{:S(2)}) async-start(f32[256,32,128]{2,1,0:T(8,128)} %get-tuple-element.6), calls=%async_computation.4 | async-start | bytes 8388608 | tf_op jit(solution)/shard_map/all_to_all | solution.py:78
  209.2 7.7 %copy-start.2 = (f32[256,32,128]{2,1,0:T(8,128)S(1)}, f32[256,32,128]{2,1,0:T(8,128)}, u32[]{:S(2)}) copy-start(f32[256,32,128]{2,1,0:T(8,128)} %get-tuple-element.5) | copy-start | bytes 12582916
  258.2 53.7 %all-to-all-start.3 = ((f32[8,32,32,128]{3,2,1,0:T(8,128)}), f32[8,32,32,128]{3,2,1,0:T(8,128)}, u32[]{:S(2)}, u32[]{:S(2)}) async-start(f32[8,32,32,128]{3,2,1,0:T(8,128)} %fusion.15), calls=%async_computation.3 | async-start | bytes 8388608 | tf_op jit(solution)/shard_map/all_to_all | solution.py:15
  314.7 4.8 %copy-start = (f32[256,32,128]{2,0,1:T(8,128)S(1)}, f32[256,32,128]{2,0,1:T(8,128)}, u32[]{:S(2)}) copy-start(f32[256,32,128]{2,0,1:T(8,128)} %fusion.27) | copy-start | bytes 12582916
  314.8 4.8 %copy-start.1 = (f32[256,32,128]{2,0,1:T(8,128)S(1)}, f32[256,32,128]{2,0,1:T(8,128)}, u32[]{:S(2)}) copy-start(f32[256,32,128]{2,0,1:T(8,128)} %fusion.29) | copy-start | bytes 12582916
